TPU v7x, 128 devices: a whole 4x4x4 slice. The times are simulated.
128 devices in a mesh: row: 16 (over z, y_lo, core), col: 8 (over x, y_hi).
Axes of the slice: x: 4, y: 4 (y_hi: 2, y_lo: 2; y = y_hi * 2 + y_lo), z: 4, core: 2. Of those that a mesh axis runs over, the one named last changes fastest.
Arguments:
- hamiltonian: float32 [8192, 8192], P(('row', 'col')), may hold values from -0.0625 to 0.0625
- coefficients: float32 [8192, 4096], P('row', 'col'), may hold values from -6 to 6
Outputs:
- applied: float32 [8192, 4096], P('row', 'col')
All inputs are finite; a program needn't handle non-finite values.
Results may differ from a plain program's by a relative error of at most 0.00007.
Values sent between devices are 32-bit elements; how exact they have to be, the bound alone decides.
A program may use at most 128 MiB of HBM per device.

v0:
```python
import jax
import jax.numpy as jnp
from jax import lax
from jax.experimental import pallas as pl
from jax.experimental.pallas import tpu as pltpu
from jax.sharding import PartitionSpec as P

MESH = pl.DeviceIdType.MESH
F32, BF16 = jnp.float32, jnp.bfloat16
SUB = 64
DEEP = 2048
WIDE = 512
SLOT = {2: 0, 1: 1, 3: 2, 0: 3}


def kernel(h_ref, c_ref, o_ref, hb, rl, cb, c3, h3, h2, hs, part, parts, r0, r13, r2, ssem, rsem, lsem):
    row, col = lax.axis_index("row"), lax.axis_index("col")
    z, yl, core = lax.div(row, 4), lax.rem(lax.div(row, 2), 2), lax.rem(row, 2)
    x, yh = lax.div(col, 2), lax.rem(col, 2)

    def device(z=z, yl=yl, core=core, x=x, yh=yh):
        return ((z * 2 + yl) * 2 + core, x * 2 + yh)

    def up(v, d):
        return lax.rem(v + d, 4)

    zp, zm = device(z=up(z, 1)), device(z=up(z, 3))
    xp, xm = device(x=up(x, 1)), device(x=up(x, 3))
    ya, yb, yc = device(yl=1 - yl), device(yl=1 - yl, yh=1 - yh), device(yh=1 - yh)
    twin = device(core=1 - core)

    barrier = pltpu.get_barrier_semaphore()
    for other in (zp, zm, xp, xm, ya, yb, yc, twin):
        pl.semaphore_signal(barrier, inc=1, device_id=other, device_id_type=MESH)
    pl.semaphore_wait(barrier, 8)

    sent, local = [], []

    def send(src, dst, to):
        n = len(sent)
        copy = pltpu.make_async_remote_copy(
            src_ref=src, dst_ref=dst, send_sem=ssem.at[n], recv_sem=rsem.at[n], device_id=to, device_id_type=MESH
        )
        copy.start()
        sent.append(copy)
        return copy

    def move(src, dst):
        copy = pltpu.make_async_copy(src, dst, lsem.at[len(local)])
        copy.start()
        local.append(copy)
        return copy

    def inner(d):
        return pl.ds(pl.multiple_of(up(z, d) * DEEP, DEEP), DEEP)

    A, B, ALL = pl.ds(0, 32), pl.ds(32, 32), pl.ds(0, 64)
    C0, C1 = pl.ds(0, 256), pl.ds(256, 256)

    to_p, to_m = {}, {}
    own_h = move(h_ref.at[:, inner(0)], hb.at[0, 0])
    own_c = move(c_ref, cb.at[0, core])
    to_p["A"] = send(h_ref.at[A, inner(1)], hb.at[0, 3, A], zp)
    to_m["A"] = send(h_ref.at[A, inner(3)], hb.at[0, 1, A], zm)
    p0, m0, p1, m1 = pl.ds(0, 48), pl.ds(16, 48), pl.ds(48, 16), pl.ds(0, 16)
    x0 = [send(h_ref.at[p0, inner(0)], hb.at[3, 0, p0], xp), send(h_ref.at[m0, inner(0)], hb.at[1, 0, m0], xm)]
    ca1 = send(c_ref.at[C1], cb.at[1, core, C1], ya)
    cb0 = send(c_ref.at[C0], cb.at[2, core, C0], yb)
    to_p["R"] = send(h_ref.at[A, inner(2)], rl.at[0], zp)
    to_m["R"] = send(h_ref.at[B, inner(2)], rl.at[1], zm)
    ca0 = send(c_ref.at[C0], cb.at[1, core, C0], ya)
    cb1 = send(c_ref.at[C1], cb.at[2, core, C1], yb)
    to_p["B"] = send(h_ref.at[B, inner(1)], hb.at[0, 3, B], zp)
    to_m["B"] = send(h_ref.at[B, inner(3)], hb.at[0, 1, B], zm)
    twins = {(0, 0): send(c_ref, cb.at[0, core], twin)}

    def split(src, rows, stores):
        def body(i, _):
            at = pl.multiple_of(i * 16, 16)
            v = src[pl.ds(at, 16), :]
            hi = v.astype(BF16)
            lo = (v - hi.astype(F32)).astype(BF16)
            for store in stores:
                store(at, hi, lo)
            return 0

        lax.fori_loop(0, rows // 16, body, 0)

    def split_h(dx, dz, batch, start, first=0, rows=SUB):
        def store(at, hi, lo):
            to = pl.ds(pl.multiple_of(start + at, 16), 16)
            h3[batch, to, pl.ds(0, DEEP)] = hi
            h3[batch, to, pl.ds(DEEP, DEEP)] = lo
            h3[batch, to, pl.ds(2 * DEEP, DEEP)] = hi

        split(hb.at[dx, dz, pl.ds(first, rows)], rows, [store])

    def stack_h(dx, dz, to, start, height, first=0, rows=SUB):
        def store(at, hi, lo):
            to[pl.ds(pl.multiple_of(start + at, 16), 16), :] = hi
            to[pl.ds(pl.multiple_of(start + height + at, 16), 16), :] = lo

        split(hb.at[dx, dz, pl.ds(first, rows)], rows, [store])

    def split_c(rel, which):
        half = 0 if rel < 2 else 1
        lower = yl if rel in (0, 3) else 1 - yl
        start = lower * 1024 + which * 512

        def store(at, hi, lo):
            to = pl.multiple_of(start + at, 16)
            c3[half, pl.ds(to, 16), :] = hi
            c3[half, pl.ds(to + DEEP, 16), :] = hi
            c3[half, pl.ds(to + 2 * DEEP, 16), :] = lo

        split(cb.at[rel, which], 512, [store])

    def multiply(batch, half, start, rows):
        def body(n, _):
            at = pl.ds(pl.multiple_of(n * 256, 256), 256)
            part[batch, half, pl.ds(start, rows), at] = jnp.dot(
                h3[batch, pl.ds(start, rows), :], c3[half, :, at], preferred_element_type=F32
            )
            return 0

        lax.fori_loop(0, 2, body, 0)

    def multiply_stack(to, stack, half):
        rows = to.shape[0]

        def body(n, _):
            at = pl.ds(pl.multiple_of(n * 256, 256), 256)
            both = jnp.dot(stack[...], c3[half, pl.ds(0, DEEP), at], preferred_element_type=F32)
            rest = jnp.dot(stack[pl.ds(0, rows), :], c3[half, pl.ds(2 * DEEP, DEEP), at], preferred_element_type=F32)
            to[:, at] = both[:rows] + both[rows:] + rest
            return 0

        lax.fori_loop(0, 2, body, 0)

    own_c.wait()
    split_c(0, core)
    own_h.wait()
    split_h(0, 0, 0, SLOT[0] * SUB)

    def along_x(dz, rows, swapped=False):
        r, l = rows[::-1] if swapped else rows, rows
        for a, b in zip(l, r):
            xs.setdefault(dz, []).extend(
                [send(hb.at[0, dz, a], hb.at[3, dz, a], xp), send(hb.at[0, dz, b], hb.at[1, dz, b], xm)]
            )

    xs = {}
    to_m["A"].wait_recv()
    along_x(1, [A])
    to_p["A"].wait_recv()
    along_x(3, [A])
    to_p["R"].wait_recv()
    far_p = send(rl.at[0], hb.at[0, 2, A], zp)
    to_m["R"].wait_recv()
    far_m = send(rl.at[1], hb.at[0, 2, B], zm)
    ca1.wait_recv()
    cc1 = send(cb.at[1, core, C1], cb.at[3, core, C1], yb)
    cb0.wait_recv()
    cc0 = send(cb.at[2, core, C0], cb.at[3, core, C0], ya)
    twins[1, 1] = send(cb.at[1, core, C1], cb.at[1, core, C1], twin)
    twins[2, 0] = send(cb.at[2, core, C0], cb.at[2, core, C0], twin)
    twins[0, 0].wait_recv()
    split_c(0, 1 - core)
    to_m["B"].wait_recv()
    along_x(1, [B])
    to_p["B"].wait_recv()
    along_x(3, [B])
    split_h(0, 1, 0, SLOT[1] * SUB)
    split_h(0, 3, 0, SLOT[3] * SUB)
    far_p.wait_recv()
    far_m.wait_recv()
    along_x(2, [A, B], swapped=True)
    ca0.wait_recv()
    twins[1, 0] = send(cb.at[1, core, C0], cb.at[1, core, C0], twin)
    cb1.wait_recv()
    twins[2, 1] = send(cb.at[2, core, C1], cb.at[2, core, C1], twin)
    split_h(0, 2, 0, SLOT[2] * SUB)
    split_c(1, core)
    twins[1, 1].wait_recv()
    twins[1, 0].wait_recv()
    split_c(1, 1 - core)

    def lies(group, dz, half, hs):
        if group == 1:
            return part.at[1 if dz in (1, 3) else 2, hs, pl.ds((128 if dz in (3, 0) else 0) + half * 64, 64), :]
        return part.at[0 if group == 0 else 3, hs, pl.ds(SLOT[dz] * 64 + half * 32, 32), :]

    def add(to, *terms):
        def body(i, _):
            at = pl.ds(pl.multiple_of(i * 8, 8), 8)
            total = terms[0][at, :]
            for term in terms[1:]:
                total = total + term[at, :]
            to[at, :] = total
            return 0

        lax.fori_loop(0, to.shape[0] // 8, body, 0)

    def add_to(to, box):
        for plane in range(to.shape[0]):
            add(to.at[plane], to.at[plane], box.at[plane])

    class Scatter:
        def __init__(self, group, box, hs):
            self.group, self.box, self.hs = group, box, hs

        def lie(self, dz, half):
            return lies(self.group, dz, half, self.hs)

        def far(self):
            self.p2 = send(self.lie(2, 0), self.box.at[0], zp)
            self.m2 = send(self.lie(2, 1), self.box.at[1], zm)

        def clean_p(self):
            self.cp = send(self.lie(1, 1), self.box.at[2], zp)

        def clean_m(self):
            self.cm = send(self.lie(3, 0), self.box.at[3], zm)

        def dirty_p(self):
            self.p2.wait_recv()
            add_to(self.lie(1, 0), self.box.at[0])
            self.dp = send(self.lie(1, 0), self.box.at[4], zp)

        def dirty_m(self):
            self.m2.wait_recv()
            add_to(self.lie(3, 1), self.box.at[1])
            self.dm = send(self.lie(3, 1), self.box.at[5], zm)

        def here(self):
            for copy in (self.cm, self.dp, self.cp, self.dm):
                copy.wait_recv()

    def rows_of(dx, first, rows):
        return pl.ds(pl.multiple_of((up(x, dx) * 2 + yh) * SUB + first, 8), rows)

    across = []

    def finish(half, terms, box, plane, dx, first, rows, side, at=0):
        came = [box.at[k, plane, pl.ds(at, rows)] for k in ((3, 4), (2, 5))[side]]
        where = rows_of(dx, first, rows)
        if half == 0:
            add(o_ref.at[where], terms, *came)
        else:
            add(terms, terms, *came)
            across.append(send(terms, o_ref.at[where], yc))

    near = [Scatter(0, r0.at[h], pl.ds(h, 1)) for h in range(2)]
    sides = [Scatter(1, r13.at[h], pl.ds(h, 1)) for h in range(2)]
    last = [Scatter(2, r2.at[h], pl.ds(h, 1)) for h in range(2)]

    multiply(0, 0, 0, 256)
    near[0].far()
    near[0].clean_p()
    near[0].clean_m()
    split_c(2, core)
    twins[2, 0].wait_recv()
    twins[2, 1].wait_recv()
    split_c(2, 1 - core)
    near[0].dirty_p()
    near[0].dirty_m()

    for dz, at in ((1, 0), (3, 128)):
        for copy in xs[dz]:
            copy.wait_recv()
        split_h(1, dz, 1, at)
        split_h(3, dz, 1, at + SUB)
    multiply(1, 0, 0, 256)
    sides[0].clean_p()
    sides[0].clean_m()
    cc1.wait_recv()
    twins[3, 1] = send(cb.at[3, core, C1], cb.at[3, core, C1], twin)
    cc0.wait_recv()
    twins[3, 0] = send(cb.at[3, core, C0], cb.at[3, core, C0], twin)
    split_c(3, core)
    twins[3, 1].wait_recv()
    twins[3, 0].wait_recv()
    split_c(3, 1 - core)

    multiply(0, 1, 0, 256)
    near[1].far()
    near[1].clean_p()
    near[1].clean_m()

    def onward(dz):
        return [send(hb.at[3, dz, A], hb.at[2, dz, A], xp), send(hb.at[1, dz, B], hb.at[2, dz, B], xm)]

    fs = {}
    for copy in xs[2][:2]:
        copy.wait_recv()
    for dz in (2, 1, 3):
        fs[dz] = onward(dz)
    for copy in x0:
        copy.wait_recv()
    fs[0] = onward(0)
    x1 = [send(hb.at[0, 0, p1], hb.at[3, 0, p1], xp), send(hb.at[0, 0, m1], hb.at[1, 0, m1], xm)]
    multiply(1, 1, 0, 256)
    sides[1].clean_p()
    sides[1].clean_m()
    near[1].dirty_p()
    near[1].dirty_m()
    for copy in xs[2][2:]:
        copy.wait_recv()
    split_h(1, 2, 2, 0)
    split_h(3, 2, 2, SUB)
    for h in (1, 0):
        multiply(2, h, 0, 128)
        sides[h].far()

    def opposite(dz):
        for copy in fs[dz]:
            copy.wait_recv()
        stack_h(2, dz, h2.at[dz], 0, SUB)

    def opposite_multiply(dz, h):
        multiply_stack(part.at[3, h, pl.ds(SLOT[dz] * 64, 64)], h2.at[dz], h)

    def finish_a(h):
        sides[h].here()
        finish(h, part.at[2, h, pl.ds(128, 48)], r13.at[h], 0, 1, 16, 48, 0, 16)
        finish(h, part.at[2, h, pl.ds(176, 48)], r13.at[h], 0, 3, 0, 48, 1, 0)

    def finish_b(h):
        multiply_stack(parts.at[h], hs, h)
        finish(h, parts.at[h, pl.ds(0, 16)], r13.at[h], 0, 1, 0, 16, 0, 0)
        finish(h, parts.at[h, pl.ds(16, 16)], r13.at[h], 0, 3, 48, 16, 1, 48)

    def finish_last(h):
        opposite_multiply(0, h)
        last[h].here()
        for side in range(2):
            finish(h, part.at[3, h, pl.ds(SLOT[0] * 64 + side * 32, 32)], r2.at[h], 0, 2, side * 32, 32, side)

    opposite(2)
    for h in (1, 0):
        opposite_multiply(2, h)
        last[h].far()
    for h in (1, 0):
        near[h].here()
        for side in range(2):
            finish(h, part.at[0, h, pl.ds(SLOT[0] * 64 + side * 32, 32)], r0.at[h], 0, 0, side * 32, 32, side)
    split_h(1, 0, 2, 128, 16, 48)
    split_h(3, 0, 2, 176, 0, 48)
    sides[1].dirty_p()
    sides[1].dirty_m()
    multiply(2, 1, 128, 96)
    sides[0].dirty_p()
    sides[0].dirty_m()
    opposite(1)
    for h in (1, 0):
        opposite_multiply(1, h)
        last[h].clean_p()
        last[h].dirty_p()
    finish_a(1)
    opposite(3)
    for h in (1, 0):
        opposite_multiply(3, h)
        last[h].clean_m()
        last[h].dirty_m()
    multiply(2, 0, 128, 96)
    finish_a(0)
    opposite(0)
    finish_last(1)
    for copy in x1:
        copy.wait_recv()
    stack_h(1, 0, hs, 0, 32, 0, 16)
    stack_h(3, 0, hs, 16, 32, 48, 16)
    finish_b(1)
    finish_last(0)
    finish_b(0)

    for copy in across:
        copy.wait_recv()
    for copy in sent:
        copy.wait_send()


def solution(mesh):
    def step(h, c):
        return pl.pallas_call(
            kernel,
            out_shape=pltpu.VMEM((512, WIDE), F32),
            in_specs=[pl.BlockSpec(memory_space=pl.ANY)] * 2,
            out_specs=pl.BlockSpec(memory_space=pltpu.VMEM),
            scratch_shapes=[
                pltpu.VMEM((4, 4, SUB, DEEP), F32),
                pltpu.VMEM((2, 32, DEEP), F32),
                pltpu.VMEM((4, 2, 512, WIDE), F32),
                pltpu.VMEM((2, 3 * DEEP, WIDE), BF16),
                pltpu.VMEM((3, 256, 3 * DEEP), BF16),
                pltpu.VMEM((4, 128, DEEP), BF16),
                pltpu.VMEM((64, DEEP), BF16),
                pltpu.VMEM((4, 2, 256, WIDE), F32),
                pltpu.VMEM((2, 32, WIDE), F32),
                pltpu.VMEM((2, 6, 1, 32, WIDE), F32),
                pltpu.VMEM((2, 6, 1, 64, WIDE), F32),
                pltpu.VMEM((2, 6, 1, 32, WIDE), F32),
                pltpu.SemaphoreType.DMA((96,)),
                pltpu.SemaphoreType.DMA((96,)),
                pltpu.SemaphoreType.DMA((2,)),
            ],
            compiler_params=pltpu.CompilerParams(collective_id=0, has_side_effects=True, vmem_limit_bytes=56 * 2**20),
        )(h, c)

    return jax.shard_map(
        step,
        mesh=mesh,
        in_specs=(P(("row", "col"), None), P("row", "col")),
        out_specs=P("row", "col"),
        check_vma=False,
    )
```

profile of v0, /device:TPU:0, one launch (start us, length us, event | category | flops | bytes accessed | tf_op | source)
XLA Modules:
  0.0 84.6 jit_solution(714154094730019571)
XLA Ops:
  0.0 83.6 %shard_map.28 = f32[512,512]{1,0:T(8,128)S(1)} custom-call(f32[64,8192]{1,0:T(8,128)} %h_ref.1, f32[512,512]{1,0:T(8,128)} %c_ref.1), custom_call_target="tpu_custom_call" | custom-call | tf_op jit(solution)/shard_map/pallas_call | solution.py:385
  83.7 1.0 %copy.4 = f32[512,512]{1,0:T(8,128)} copy(f32[512,512]{1,0:T(8,128)S(1)} %shard_map.28) | data formatting | bytes 2097152
where the time goes:
time: 84.8 us; the launch traced here: 84.6 us
  Pallas kernels  83.6 us (99%)
  local copies, waits for them, and re-layouts  0.97 us (1%)
    pallas_call x1, Pallas kernels, step(): pl.pallas_call(kernel, out_shape=pltpu.VMEM((512, WIDE), F32), in_specs=[...  83.6 us

commit v1 on v0

v1 whole, which is shorter than its diff:
```python
import jax
import jax.numpy as jnp
from jax import lax
from jax.experimental import pallas as pl
from jax.experimental.pallas import tpu as pltpu
from jax.sharding import PartitionSpec as P

MESH = pl.DeviceIdType.MESH
F32, BF16 = jnp.float32, jnp.bfloat16
SUB = 64
DEEP = 2048
WIDE = 512
SLOT = {2: 0, 1: 1, 3: 2, 0: 3}
ROWS, ORBITALS, TWIN, SUMS, HALVES = range(5)
GROUPS = 46


def kernel(h_ref, c_ref, o_ref, hb, rl, cb, c3, h3, h2, ha, he, hz, part, pa, pe, pz, r0, r13, r2, ssem, rsem, lsem):
    row, col = lax.axis_index("row"), lax.axis_index("col")
    z, yl, core = lax.div(row, 4), lax.rem(lax.div(row, 2), 2), lax.rem(row, 2)
    x, yh = lax.div(col, 2), lax.rem(col, 2)

    def device(z=z, yl=yl, core=core, x=x, yh=yh):
        return ((z * 2 + yl) * 2 + core, x * 2 + yh)

    def up(v, d):
        return lax.rem(v + d, 4)

    zp, zm = device(z=up(z, 1)), device(z=up(z, 3))
    xp, xm = device(x=up(x, 1)), device(x=up(x, 3))
    ya, yb, yc = device(yl=1 - yl), device(yl=1 - yl, yh=1 - yh), device(yh=1 - yh)
    twin = device(core=1 - core)

    barrier = pltpu.get_barrier_semaphore()
    for other in (zp, zm, xp, xm, ya, yb, yc, twin):
        pl.semaphore_signal(barrier, inc=1, device_id=other, device_id_type=MESH)
    pl.semaphore_wait(barrier, 8)

    local, groups = [], []

    def group():
        groups.append(None)
        return rsem.at[len(groups) - 1]

    def send(src, dst, to, kind, into=None):
        copy = pltpu.make_async_remote_copy(
            src_ref=src,
            dst_ref=dst,
            send_sem=ssem.at[kind],
            recv_sem=group() if into is None else into,
            device_id=to,
            device_id_type=MESH,
        )
        copy.start()
        return copy

    def wait_for(like, sem):
        pltpu.make_async_copy(like, like, sem).wait()

    def move(src, dst):
        copy = pltpu.make_async_copy(src, dst, lsem.at[len(local)])
        copy.start()
        local.append(copy)
        return copy

    def inner(d):
        return pl.ds(pl.multiple_of(up(z, d) * DEEP, DEEP), DEEP)

    A, B, ALL = pl.ds(0, 32), pl.ds(32, 32), pl.ds(0, 64)
    C0, C1 = pl.ds(0, 256), pl.ds(256, 256)

    to_p, to_m = {}, {}
    own_h = move(h_ref.at[:, inner(0)], hb.at[0, 0])
    own_c = move(c_ref, cb.at[0, core])
    to_p["A"] = send(h_ref.at[A, inner(1)], hb.at[0, 3, A], zp, ROWS)
    to_m["A"] = send(h_ref.at[A, inner(3)], hb.at[0, 1, A], zm, ROWS)
    p0, m0 = pl.ds(0, 48), pl.ds(16, 48)
    x0 = group()
    send(h_ref.at[p0, inner(0)], hb.at[3, 0, p0], xp, ROWS, x0)
    send(h_ref.at[m0, inner(0)], hb.at[1, 0, m0], xm, ROWS, x0)
    ca1 = send(c_ref.at[C1], cb.at[1, core, C1], ya, ORBITALS)
    cb0 = send(c_ref.at[C0], cb.at[2, core, C0], yb, ORBITALS)
    to_p["R"] = send(h_ref.at[A, inner(2)], rl.at[0], zp, ROWS)
    to_m["R"] = send(h_ref.at[B, inner(2)], rl.at[1], zm, ROWS)
    ca0 = send(c_ref.at[C0], cb.at[1, core, C0], ya, ORBITALS)
    cb1 = send(c_ref.at[C1], cb.at[2, core, C1], yb, ORBITALS)
    to_p["B"] = send(h_ref.at[B, inner(1)], hb.at[0, 3, B], zp, ROWS)
    to_m["B"] = send(h_ref.at[B, inner(3)], hb.at[0, 1, B], zm, ROWS)
    own_twin = send(c_ref, cb.at[0, core], twin, TWIN)

    def split(src, rows, stores):
        def body(i, _):
            at = pl.multiple_of(i * 16, 16)
            v = src[pl.ds(at, 16), :]
            hi = v.astype(BF16)
            lo = (v - hi.astype(F32)).astype(BF16)
            for store in stores:
                store(at, hi, lo)
            return 0

        lax.fori_loop(0, rows // 16, body, 0)

    def split_h(dx, dz, batch, start, first=0, rows=SUB):
        def store(at, hi, lo):
            to = pl.ds(pl.multiple_of(start + at, 16), 16)
            h3[batch, to, pl.ds(0, DEEP)] = hi
            h3[batch, to, pl.ds(DEEP, DEEP)] = lo
            h3[batch, to, pl.ds(2 * DEEP, DEEP)] = hi

        split(hb.at[dx, dz, pl.ds(first, rows)], rows, [store])

    def stack_h(dx, dz, to, start, height, first=0, rows=SUB):
        def store(at, hi, lo):
            to[pl.ds(pl.multiple_of(start + at, 16), 16), :] = hi
            to[pl.ds(pl.multiple_of(start + height + at, 16), 16), :] = lo

        split(hb.at[dx, dz, pl.ds(first, rows)], rows, [store])

    def stack_pair(first, second, to, start, height):
        v = jnp.concatenate([first[...], second[...]], axis=0)
        hi = v.astype(BF16)
        to[pl.ds(start, 16), :] = hi
        to[pl.ds(start + height, 16), :] = (v - hi.astype(F32)).astype(BF16)

    def split_c(rel, which):
        half = 0 if rel < 2 else 1
        lower = yl if rel in (0, 3) else 1 - yl
        start = lower * 1024 + which * 512

        def store(at, hi, lo):
            to = pl.multiple_of(start + at, 16)
            c3[half, pl.ds(to, 16), :] = hi
            c3[half, pl.ds(to + DEEP, 16), :] = hi
            c3[half, pl.ds(to + 2 * DEEP, 16), :] = lo

        split(cb.at[rel, which], 512, [store])

    def multiply(batch, half, start, rows):
        def body(n, _):
            at = pl.ds(pl.multiple_of(n * 256, 256), 256)
            part[batch, half, pl.ds(start, rows), at] = jnp.dot(
                h3[batch, pl.ds(start, rows), :], c3[half, :, at], preferred_element_type=F32
            )
            return 0

        lax.fori_loop(0, 2, body, 0)

    def multiply_stack(to, stack, half, tiles=None):
        rows = to.shape[0]

        def body(n, _):
            at = pl.ds(pl.multiple_of(n * 256, 256), 256)
            both = jnp.dot(stack[...], c3[half, pl.ds(0, DEEP), at], preferred_element_type=F32)
            rest = jnp.dot(stack[pl.ds(0, rows), :], c3[half, pl.ds(2 * DEEP, DEEP), at], preferred_element_type=F32)
            to[:, at] = both[:rows] + both[rows:] + rest
            return 0

        if tiles is None:
            lax.fori_loop(0, 2, body, 0)
        else:
            body(tiles, 0)

    own_c.wait()
    split_c(0, core)
    own_h.wait()
    split_h(0, 0, 0, SLOT[0] * SUB)

    def along_x(dz, a, b, sem):
        send(hb.at[0, dz, a], hb.at[3, dz, a], xp, ROWS, sem)
        send(hb.at[0, dz, b], hb.at[1, dz, b], xm, ROWS, sem)

    xs = {dz: group() for dz in range(4)}
    twins = {rel: group() for rel in (1, 2, 3)}
    to_m["A"].wait_recv()
    along_x(1, A, A, xs[1])
    to_p["A"].wait_recv()
    along_x(3, A, A, xs[3])
    to_p["R"].wait_recv()
    far_p = send(rl.at[0], hb.at[0, 2, A], zp, ROWS)
    to_m["R"].wait_recv()
    far_m = send(rl.at[1], hb.at[0, 2, B], zm, ROWS)
    ca1.wait_recv()
    cc1 = send(cb.at[1, core, C1], cb.at[3, core, C1], yb, ORBITALS)
    cb0.wait_recv()
    cc0 = send(cb.at[2, core, C0], cb.at[3, core, C0], ya, ORBITALS)
    send(cb.at[1, core, C1], cb.at[1, core, C1], twin, TWIN, twins[1])
    send(cb.at[2, core, C0], cb.at[2, core, C0], twin, TWIN, twins[2])
    own_twin.wait_recv()
    split_c(0, 1 - core)
    to_m["B"].wait_recv()
    along_x(1, B, B, xs[1])
    to_p["B"].wait_recv()
    split_h(0, 1, 0, SLOT[1] * SUB)
    split_h(0, 3, 0, SLOT[3] * SUB)
    far_p.wait_recv()
    far_m.wait_recv()
    along_x(2, A, B, xs[0])
    along_x(2, B, A, xs[2])
    along_x(3, B, B, xs[3])
    ca0.wait_recv()
    send(cb.at[1, core, C0], cb.at[1, core, C0], twin, TWIN, twins[1])
    cb1.wait_recv()
    send(cb.at[2, core, C1], cb.at[2, core, C1], twin, TWIN, twins[2])
    split_h(0, 2, 0, SLOT[2] * SUB)
    split_c(1, core)
    wait_for(cb.at[0, 0], twins[1])
    split_c(1, 1 - core)

    def lies(group, dz, half, hs):
        if group == 1:
            return part.at[1 if dz in (1, 3) else 2, hs, pl.ds((128 if dz in (3, 0) else 0) + half * 64, 64), :]
        return part.at[0 if group == 0 else 3, hs, pl.ds(SLOT[dz] * 64 + half * 32, 32), :]

    def add(to, *terms):
        def body(i, _):
            at = pl.ds(pl.multiple_of(i * 8, 8), 8)
            total = terms[0][at, :]
            for term in terms[1:]:
                total = total + term[at, :]
            to[at, :] = total
            return 0

        lax.fori_loop(0, to.shape[0] // 8, body, 0)

    def add_to(to, box):
        for plane in range(to.shape[0]):
            add(to.at[plane], to.at[plane], box.at[plane])

    class Scatter:
        def __init__(self, which, box, hs):
            self.group, self.box, self.hs, self.sem = which, box, hs, group()

        def lie(self, dz, half):
            return lies(self.group, dz, half, self.hs)

        def far(self):
            self.p2 = send(self.lie(2, 0), self.box.at[0], zp, SUMS)
            self.m2 = send(self.lie(2, 1), self.box.at[1], zm, SUMS)

        def clean_p(self):
            send(self.lie(1, 1), self.box.at[2], zp, SUMS, self.sem)

        def clean_m(self):
            send(self.lie(3, 0), self.box.at[3], zm, SUMS, self.sem)

        def dirty_p(self):
            self.p2.wait_recv()
            add_to(self.lie(1, 0), self.box.at[0])
            send(self.lie(1, 0), self.box.at[4], zp, SUMS, self.sem)

        def dirty_m(self):
            self.m2.wait_recv()
            add_to(self.lie(3, 1), self.box.at[1])
            send(self.lie(3, 1), self.box.at[5], zm, SUMS, self.sem)

        def here(self):
            wait_for(part.at[0, 0, pl.ds(0, 4 * self.box.shape[2])], self.sem)

    class OneWay:
        def __init__(self, box, h):
            self.box, self.sem, self.at = box, group(), [part.at[3, h, pl.ds(SLOT[dz] * 64, 64)] for dz in range(4)]

        def far(self):
            self.f = send(self.at[2], self.box.at[0], zp, SUMS)

        def upper(self):
            self.f.wait_recv()
            add(self.at[1], self.at[1], self.box.at[0])
            send(self.at[1], self.box.at[1], zp, SUMS, self.sem)

        def lower(self):
            send(self.at[3], self.box.at[2], zm, SUMS, self.sem)

        def here(self):
            wait_for(part.at[0, 0, pl.ds(0, 128)], self.sem)

    def rows_of(dx, first, rows):
        return pl.ds(pl.multiple_of((up(x, dx) * 2 + yh) * SUB + first, 8), rows)

    across = group()

    def finish(half, terms, box, dx, first, rows, side, at=0, cols=pl.ds(0, WIDE)):
        planes = (3, 4), (2, 5)
        if side is None:
            came = [box.at[k, pl.ds(at, rows), cols] for k in (1, 2)]
        else:
            came = [box.at[k, 0, pl.ds(at, rows), cols] for k in planes[side]]
        where = rows_of(dx, first, rows)
        if half == 0:
            add(o_ref.at[where, cols], terms, *came)
        else:
            add(terms, terms, *came)
            send(terms, o_ref.at[where, cols], yc, HALVES, across)

    near = [Scatter(0, r0.at[h], pl.ds(h, 1)) for h in range(2)]
    sides = [Scatter(1, r13.at[h], pl.ds(h, 1)) for h in range(2)]
    last = [OneWay(r2.at[h], h) for h in range(2)]

    multiply(0, 0, 0, 256)
    near[0].far()
    near[0].clean_p()
    near[0].clean_m()
    split_c(2, core)
    wait_for(cb.at[0, 0], twins[2])
    split_c(2, 1 - core)
    near[0].dirty_p()
    near[0].dirty_m()

    def beside(dz, batch, start):
        wait_for(hb.at[0, 0] if dz == 2 else hb.at[pl.ds(0, 2), 0], xs[dz])
        split_h(1, dz, batch, start)
        split_h(3, dz, batch, start + SUB)

    beside(1, 1, 0)
    multiply(1, 0, 0, 128)
    sides[0].clean_p()
    cc1.wait_recv()
    send(cb.at[3, core, C1], cb.at[3, core, C1], twin, TWIN, twins[3])
    cc0.wait_recv()
    send(cb.at[3, core, C0], cb.at[3, core, C0], twin, TWIN, twins[3])
    split_c(3, core)
    wait_for(cb.at[0, 0], twins[3])
    split_c(3, 1 - core)

    multiply(0, 1, 0, 256)
    near[1].far()
    near[1].clean_p()
    near[1].clean_m()

    def onward(dz, a, b, sem):
        send(hb.at[3, dz, a], hb.at[2, dz, a], xp, ROWS, sem)
        send(hb.at[1, dz, b], hb.at[2, dz, b], xm, ROWS, sem)
        return sem

    fs = {}
    wait_for(hb.at[0, 0], xs[0])
    fs[2] = onward(2, A, B, group())
    fs[1] = onward(1, A, B, group())
    beside(2, 2, 0)
    multiply(2, 1, 0, 128)
    sides[1].far()
    multiply(1, 1, 0, 128)
    sides[1].clean_p()
    multiply(2, 0, 0, 128)
    near[1].dirty_p()
    near[1].dirty_m()
    beside(3, 1, 128)
    fs[3] = onward(3, A, B, group())
    wait_for(hb.at[pl.ds(0, 2), 0, pl.ds(0, 48)], x0)

    def rest(a, b, sem):
        send(hb.at[0, 0, a], hb.at[3, 0, a], xp, ROWS, sem)
        send(hb.at[0, 0, b], hb.at[1, 0, b], xm, ROWS, sem)

    early, late, end = group(), group(), group()
    rest(pl.ds(48, 8), pl.ds(8, 8), early)
    onward(0, pl.ds(0, 16), pl.ds(32, 16), early)
    onward(0, pl.ds(16, 16), pl.ds(48, 16), late)
    rest(pl.ds(56, 8), pl.ds(0, 8), end)
    multiply(1, 1, 128, 128)
    sides[1].clean_m()
    sides[1].dirty_p()
    sides[1].dirty_m()
    multiply(1, 0, 128, 128)
    split_h(1, 0, 2, 128, 16, 48)
    split_h(3, 0, 2, 176, 0, 48)
    multiply(2, 1, 128, 96)

    def opposite(dz):
        wait_for(hb.at[0, 0], fs[dz])
        stack_h(2, dz, h2.at[dz], 0, SUB)

    def opposite_multiply(dz, h):
        multiply_stack(part.at[3, h, pl.ds(SLOT[dz] * 64, 64)], h2.at[dz], h)

    def finish_a(h):
        sides[h].here()
        finish(h, part.at[2, h, pl.ds(128, 48)], r13.at[h], 1, 16, 48, 0, 16)
        finish(h, part.at[2, h, pl.ds(176, 48)], r13.at[h], 3, 0, 48, 1, 0)

    def finish_early(h):
        finish(h, pa.at[h, pl.ds(0, 16)], r2.at[h], 2, 0, 16, None, 0)
        finish(h, pa.at[h, pl.ds(16, 16)], r2.at[h], 2, 32, 16, None, 32)

    def finish_side(h):
        finish(h, pa.at[h, pl.ds(32, 8)], r13.at[h], 1, 8, 8, 0, 8)
        finish(h, pa.at[h, pl.ds(40, 8)], r13.at[h], 3, 48, 8, 1, 48)

    def finish_late(h):
        finish(h, pe.at[h, pl.ds(0, 16)], r2.at[h], 2, 16, 16, None, 16)
        finish(h, pe.at[h, pl.ds(16, 16)], r2.at[h], 2, 48, 16, None, 48)

    def finish_end(h, cols):
        finish(h, pz.at[h, pl.ds(0, 8), cols], r13.at[h], 1, 0, 8, 0, 0, cols)
        finish(h, pz.at[h, pl.ds(8, 8), cols], r13.at[h], 3, 56, 8, 1, 56, cols)

    opposite(2)
    opposite_multiply(2, 1)
    last[1].far()
    sides[0].far()
    sides[0].clean_m()
    opposite_multiply(2, 0)
    multiply(2, 0, 128, 96)
    opposite(1)
    opposite_multiply(1, 1)
    last[1].upper()
    last[0].far()
    finish_a(1)
    sides[0].dirty_m()
    opposite_multiply(1, 0)
    for h in (1, 0):
        near[h].here()
        for side in range(2):
            finish(h, part.at[0, h, pl.ds(SLOT[0] * 64 + side * 32, 32)], r0.at[h], 0, side * 32, 32, side)
    sides[0].dirty_p()
    opposite(3)
    opposite_multiply(3, 1)
    last[1].lower()
    opposite_multiply(3, 0)
    last[0].lower()
    wait_for(hb.at[0, 0, pl.ds(0, 48)], early)
    stack_h(2, 0, ha, 0, 48, 0, 16)
    stack_h(2, 0, ha, 16, 48, 32, 16)
    stack_pair(hb.at[1, 0, pl.ds(8, 8)], hb.at[3, 0, pl.ds(48, 8)], ha, 32, 48)
    multiply_stack(pa.at[1], ha, 1)
    finish_side(1)
    last[1].here()
    finish_early(1)
    last[0].upper()
    wait_for(hb.at[0, 0, pl.ds(0, 32)], late)
    stack_h(2, 0, he, 0, 32, 16, 16)
    stack_h(2, 0, he, 16, 32, 48, 16)
    multiply_stack(pe.at[1], he, 1)
    finish_late(1)
    wait_for(hb.at[0, 0, pl.ds(0, 16)], end)
    stack_pair(hb.at[1, 0, pl.ds(0, 8)], hb.at[3, 0, pl.ds(56, 8)], hz, 0, 16)
    for n in range(2):
        multiply_stack(pz.at[1], hz, 1, n)
        finish_end(1, pl.ds(n * 256, 256))
    multiply_stack(pa.at[0], ha, 0)
    multiply_stack(pe.at[0], he, 0)
    finish_a(0)
    finish_side(0)
    multiply_stack(pz.at[0], hz, 0)
    finish_end(0, pl.ds(0, WIDE))
    last[0].here()
    finish_early(0)
    finish_late(0)

    wait_for(hb, ssem.at[ROWS])
    wait_for(cb.at[pl.ds(0, 3), 0], ssem.at[ORBITALS])
    wait_for(cb.at[pl.ds(0, 4), 0], ssem.at[TWIN])
    wait_for(part.at[pl.ds(0, 3)], ssem.at[SUMS])
    wait_for(o_ref.at[pl.ds(0, 256)], ssem.at[HALVES])
    wait_for(o_ref.at[pl.ds(0, 256)], across)


def solution(mesh):
    def step(h, c):
        return pl.pallas_call(
            kernel,
            out_shape=pltpu.VMEM((512, WIDE), F32),
            in_specs=[pl.BlockSpec(memory_space=pl.ANY)] * 2,
            out_specs=pl.BlockSpec(memory_space=pltpu.VMEM),
            scratch_shapes=[
                pltpu.VMEM((4, 4, SUB, DEEP), F32),
                pltpu.VMEM((2, 32, DEEP), F32),
                pltpu.VMEM((4, 2, 512, WIDE), F32),
                pltpu.VMEM((2, 3 * DEEP, WIDE), BF16),
                pltpu.VMEM((3, 256, 3 * DEEP), BF16),
                pltpu.VMEM((4, 128, DEEP), BF16),
                pltpu.VMEM((96, DEEP), BF16),
                pltpu.VMEM((64, DEEP), BF16),
                pltpu.VMEM((32, DEEP), BF16),
                pltpu.VMEM((4, 2, 256, WIDE), F32),
                pltpu.VMEM((2, 48, WIDE), F32),
                pltpu.VMEM((2, 32, WIDE), F32),
                pltpu.VMEM((2, 16, WIDE), F32),
                pltpu.VMEM((2, 6, 1, 32, WIDE), F32),
                pltpu.VMEM((2, 6, 1, 64, WIDE), F32),
                pltpu.VMEM((2, 3, 64, WIDE), F32),
                pltpu.SemaphoreType.DMA((5,)),
                pltpu.SemaphoreType.DMA((GROUPS,)),
                pltpu.SemaphoreType.DMA((2,)),
            ],
            compiler_params=pltpu.CompilerParams(collective_id=0, has_side_effects=True, vmem_limit_bytes=56 * 2**20),
        )(h, c)

    return jax.shard_map(
        step,
        mesh=mesh,
        in_specs=(P(("row", "col"), None), P("row", "col")),
        out_specs=P("row", "col"),
        check_vma=False,
    )
```

time: 84.8 us -> 83.1 us (0.980)
  Pallas kernels: 83.6 us -> 82 us
    pallas_call x1, Pallas kernels: 83.6 us -> 82 us  [step(): pl.pallas_call(kernel, out_shape=pltpu.VMEM((512, WIDE), F32), in_specs=[...]
where the time goes in v1:
time: 83.1 us; the launch traced here: 82.9 us
  Pallas kernels  82 us (99%)
  local copies, waits for them, and re-layouts  0.97 us (1%)
    pallas_call x1, Pallas kernels, step(): pl.pallas_call(kernel, out_shape=pltpu.VMEM((512, WIDE), F32), in_specs=[...  82 us

profile of v1, /device:TPU:0, one launch (start us, length us, event | category | flops | bytes accessed | tf_op | source)
XLA Modules:
  0.0 82.9 jit_solution(15604525404594612961)
XLA Ops:
  0.0 82.0 %shard_map.28 = f32[512,512]{1,0:T(8,128)S(1)} custom-call(f32[64,8192]{1,0:T(8,128)} %h_ref.1, f32[512,512]{1,0:T(8,128)} %c_ref.1), custom_call_target="tpu_custom_call" | custom-call | tf_op jit(solution)/shard_map/pallas_call | solution.py:460
  82.0 1.0 %copy.4 = f32[512,512]{1,0:T(8,128)} copy(f32[512,512]{1,0:T(8,128)S(1)} %shard_map.28) | data formatting | bytes 2097152

commit v2 on v1

--- a/solution.py
+++ b/solution.py
@@ -145,20 +145,13 @@
 
         lax.fori_loop(0, 2, body, 0)
 
-    def multiply_stack(to, stack, half, tiles=None):
+    def multiply_stack(to, stack, half, tile=None):
         rows = to.shape[0]
 
-        def body(n, _):
-            at = pl.ds(pl.multiple_of(n * 256, 256), 256)
-            both = jnp.dot(stack[...], c3[half, pl.ds(0, DEEP), at], preferred_element_type=F32)
-            rest = jnp.dot(stack[pl.ds(0, rows), :], c3[half, pl.ds(2 * DEEP, DEEP), at], preferred_element_type=F32)
-            to[:, at] = both[:rows] + both[rows:] + rest
-            return 0
-
-        if tiles is None:
-            lax.fori_loop(0, 2, body, 0)
-        else:
-            body(tiles, 0)
+        at = pl.ds(0, WIDE) if tile is None else pl.ds(tile * 256, 256)
+        both = jnp.dot(stack[...], c3[half, pl.ds(0, DEEP), at], preferred_element_type=F32)
+        rest = jnp.dot(stack[pl.ds(0, rows), :], c3[half, pl.ds(2 * DEEP, DEEP), at], preferred_element_type=F32)
+        to[:, at] = both[:rows] + both[rows:] + rest
 
     own_c.wait()
     split_c(0, core)

time: 83.1 us -> 82.9 us (level)
  no operation moved by 1% of the time
where the time goes in v2:
time: 82.9 us; the launch traced here: 82.8 us
  Pallas kernels  81.8 us (99%)
  local copies, waits for them, and re-layouts  0.97 us (1%)
    pallas_call x1, Pallas kernels, step(): pl.pallas_call(kernel, out_shape=pltpu.VMEM((512, WIDE), F32), in_specs=[...  81.8 us

profile of v2, /device:TPU:0, one launch (start us, length us, event | category | flops | bytes accessed | tf_op | source)
XLA Modules:
  0.0 82.8 jit_solution(7065808634897376250)
XLA Ops:
  0.0 81.8 %shard_map.28 = f32[512,512]{1,0:T(8,128)S(1)} custom-call(f32[64,8192]{1,0:T(8,128)} %h_ref.1, f32[512,512]{1,0:T(8,128)} %c_ref.1), custom_call_target="tpu_custom_call" | custom-call | tf_op jit(solution)/shard_map/pallas_call | solution.py:453
  81.8 1.0 %copy.4 = f32[512,512]{1,0:T(8,128)} copy(f32[512,512]{1,0:T(8,128)S(1)} %shard_map.28) | data formatting | bytes 2097152
